TPU v7x, 32 devices: a whole 2x2x4 slice. The times are simulated.
32 devices in a mesh: row: 8 (over z, x), col: 4 (over y, core).
Axes of the slice: x: 2, y: 2, z: 4, core: 2. Of those that a mesh axis runs over, the one named last changes fastest.
Arguments:
- dense_a: bfloat16 [64, 512, 512], P(('row', 'col')), may hold values from -6 to 6
- dense_b: bfloat16 [64, 512, 512], P(('row', 'col')), may hold values from -0.25 to 0.25
- inner_basis_stack: bfloat16 [64, 2, 512, 128], P(('row', 'col')), may hold values from -0.25 to 0.25
- outer_basis_stack: bfloat16 [64, 2, 512, 128], P(('row', 'col')), may hold values from -1 to 1
- ascent: bfloat16 [32, 4, 2, 128, 128], P(('row', 'col')), may hold values from -0.4375 to 0.4375
- descent: bfloat16 [32, 4, 2, 128, 128], P(('row', 'col')), may hold values from -0.5 to 0.5
- couplings: bfloat16 [32, 2, 4, 128, 128], P(('row', 'col')), may hold values from -0.5 to 0.5
Outputs:
- product_diag: bfloat16 [64, 512, 512], P(('row', 'col'))
All inputs are finite; a program needn't handle non-finite values.
Results may differ from a plain program's by a relative error of at most 0.015.
Values may be sent and summed in bfloat16 or wider, within the bound.
A program may use at most 64 MiB of HBM per device.

v0:
```python
import jax
import jax.numpy as jnp
from jax import lax
from jax.sharding import PartitionSpec as P

HIGHEST_PRECISION = lax.Precision.HIGHEST


def from_partner(block, axis, distance):
    count = lax.axis_size(axis)
    route = []
    for low in range(count):
        high = low | 1 << distance
        if high != low and high < count:
            route += [(low, high), (high, low)]
    return lax.ppermute(block, axis, route)


def multiply(first_arg, second_arg):
    return jnp.matmul(
        first_arg.astype(jnp.float32), second_arg.astype(jnp.float32), precision=HIGHEST_PRECISION
    )


def lifted(pair_stack, inner_value):
    return multiply(multiply(jnp.swapaxes(pair_stack[:, 0], 1, 2), inner_value), pair_stack[:, 1])


def lowered(pair_stack, parent):
    return multiply(multiply(pair_stack[:, 0], parent), jnp.swapaxes(pair_stack[:, 1], 1, 2))


def lift_single(up_pair, inner_value):
    return multiply(multiply(up_pair[0].T, inner_value), up_pair[1])


def lower_single(down_pair, parent):
    return multiply(multiply(down_pair[0], parent), down_pair[1].T)


def sibling_terms(blocks, inner_value):
    left_terms = multiply(multiply(blocks[:, 0], inner_value[1::2]), blocks[:, 3])
    right_terms = multiply(multiply(blocks[:, 1], inner_value[0::2]), blocks[:, 2])
    return jnp.stack([left_terms, right_terms], 1).reshape(inner_value.shape)


def ancestor_owners(position, levels):
    powers = 2 ** jnp.arange(levels, dtype=jnp.int32)
    return position // (2 * powers) * (2 * powers) + powers - 1


def shards(dense_a, dense_b, inner_basis_stack, outer_basis_stack, ascent, descent, couplings):
    rank_size = ascent.shape[-1]
    up_pairs = ascent[0]
    down_pairs = descent[0]
    blocks = couplings[0]
    leaf_inner_product = jnp.einsum(
        "ufw,ufa->uwa",
        inner_basis_stack[:, 0],
        inner_basis_stack[:, 1],
        preferred_element_type=jnp.float32,
    )
    leaf_terms = lifted(up_pairs[0:2], leaf_inner_product)
    node_inner = leaf_terms[0] + leaf_terms[1]
    node_term = lift_single(up_pairs[2], node_inner)
    levels = (lax.axis_size("row") * lax.axis_size("col")).bit_length() - 1
    position = lax.axis_index(("row", "col"))
    own_gens = jnp.concatenate([up_pairs[3], down_pairs[3], blocks[1]], 0)
    owner_list = ancestor_owners(position, levels)
    sibling_inner = []
    first_height = 1
    holder = (owner_list == position)[:, None, None, None]
    table = jnp.where(holder, own_gens[None], jnp.zeros_like(own_gens)[None])
    for height in range(first_height, levels + 1):
        upper_part = table[height - 1 :]
        outgoing = jnp.stack([node_inner, node_term])
        received = from_partner(outgoing, ("row", "col"), height - 1)
        got_gens = from_partner(upper_part, ("row", "col"), height - 1)
        table = jnp.concatenate([table[: height - 1], upper_part + got_gens], 0)
        sibling_inner.append(received[0])
        node_inner = node_term + received[1]
        if height < levels:
            node_term = lift_single(table[height - 1, 0:2], node_inner)
    own_coupling = jnp.zeros((rank_size, rank_size), jnp.float32)
    for height in range(levels, 0, -1):
        blocks_here = table[height - 1, 4:8]
        on_left = position // 2 ** (height - 1) % 2 == 0
        first_block = jnp.where(on_left, blocks_here[0], blocks_here[1])
        second_block = jnp.where(on_left, blocks_here[3], blocks_here[2])
        near_value = multiply(multiply(first_block, sibling_inner[height - 1]), second_block)
        if height >= 2:
            down_here = table[height - 2, 2:4]
        else:
            down_here = down_pairs[2]
        own_coupling = near_value + lower_single(down_here, own_coupling)
    near_leaves = sibling_terms(blocks[0][None], leaf_inner_product)
    spread_leaves = jnp.broadcast_to(own_coupling, (2, rank_size, rank_size))
    leaf_coupling = near_leaves + lowered(down_pairs[0:2], spread_leaves)
    rounded_count = leaf_coupling.astype(jnp.bfloat16)
    spread_rows = jnp.einsum(
        "ywv,yvu->ywu", outer_basis_stack[:, 0], rounded_count, preferred_element_type=jnp.float32
    ).astype(jnp.bfloat16)
    result_block = jnp.einsum("lij,ljk->lik", dense_a, dense_b, preferred_element_type=jnp.float32)
    result_block = result_block + jnp.einsum(
        "lms,lns->lmn", spread_rows, outer_basis_stack[:, 1], preferred_element_type=jnp.float32
    )
    return result_block.astype(jnp.bfloat16)


def solution(mesh):
    placed = (
        P(("row", "col"), None, None),
        P(("row", "col"), None, None),
        P(("row", "col"), None, None, None),
        P(("row", "col"), None, None, None),
        P(("row", "col"), None, None, None, None),
        P(("row", "col"), None, None, None, None),
        P(("row", "col"), None, None, None, None),
    )
    return jax.shard_map(
        shards, mesh=mesh, in_specs=placed, out_specs=P(("row", "col"), None, None), check_vma=False
    )
```

profile of v0, /device:TPU:0, one launch (start us, length us, event | category | flops | bytes accessed | tf_op | source)
XLA Modules:
  0.0 102.3 jit_solution(17633469322373703952)
XLA Ops:
  0.0 0.1 add_compare_fusion
  0.1 0.9 slice_bitcast_fusion.30
  1.1 0.8 slice_bitcast_fusion.29
  1.9 1.0 %slice_bitcast_fusion.2 = (bf16[1,4,128,128]{3,2,1,0:T(8,128)(2,1)S(1)}, bf16[4,128,128]{2,1,0:T(8,128)(2,1)S(1)}) fusion(bf16[1,2,4,128,128]{4,3,2,1,0:T(8,128)(2,1)} %param.13), kind=kLoop, calls=%fused_computation.33 | loop fusion | bytes 524288 | tf_op jit(solution)/shard_map/slice | solution.py:96
  3.0 1.2 %broadcast_select_fusion = bf16[5,8,128,128]{3,2,1,0:T(8,128)(2,1)} fusion(pred[5]{0:T(512)(128)(4,1)S(1)} %add_compare_fusion, bf16[8,128,128]{2,1,0:T(8,128)(2,1)S(1)} %pad_maximum_fusion), kind=kLoop, calls=%fused_computation.1 | loop fusion | flops 655360 | bytes 1572869 | tf_op jit(solution)/shard_map/jit(_where)/select_n | solution.py:73
  4.2 0.5 collective-permute-start
  4.8 0.3 fusion.2
  5.0 0.3 fusion.24
  5.3 0.2 fusion.23
  5.5 0.2 fusion.27
  5.8 0.3 fusion.80
  6.2 0.2 fusion.26
  6.5 0.2 convolution_bitcast_fusion.2
  6.7 0.2 fusion.25
  7.0 0.2 convolution_bitcast_fusion.1
  7.3 0.3 collective-permute-done
  7.6 0.2 fusion.30
  7.8 0.1 slice.506
  7.9 2.9 %collective-permute-start.2 = (bf16[4,8,128,128]{3,2,1,0:T(8,128)(2,1)S(1)}, bf16[4,8,128,128]{3,2,1,0:T(8,128)(2,1)S(1)}, u32[]{:S(2)}, u32[]{:S(2)}) collective-permute-start(bf16[4,8,128,128]{3,2,1,0:T(8,128)(2,1)S(1)} %slice.506), channel_id=1, source_target_pairs={{0,2},{2,0},{1,3},{3,1},{4,6},{6,4},{5,7},{7,5},{8,10},{10,8},{9,1... | collective-permute-start | bytes 3145736 | tf_op jit(solution)/shard_map/ppermute | solution.py:16
  10.9 0.2 fusion.66
  11.1 0.2 fusion.65
  11.4 0.2 fusion.22
  11.6 25.5 %collective-permute-done.3 = f32[2,128,128]{2,1,0:T(8,128)S(1)} collective-permute-done((f32[2,128,128]{2,1,0:T(8,128)S(1)}, f32[2,128,128]{2,1,0:T(8,128)S(1)}, u32[]{:S(2)}, u32[]{:S(2)}) %collective-permute-start.3) | collective-permute-done | bytes 131104 | tf_op jit(solution)/shard_map/ppermute | solution.py:16
  37.1 0.1 slice_add_fusion.4
  37.3 1.8 %collective-permute-start.4 = (bf16[3,8,128,128]{3,2,1,0:T(8,128)(2,1)S(1)}, bf16[3,8,128,128]{3,2,1,0:T(8,128)(2,1)S(1)}, u32[]{:S(2)}, u32[]{:S(2)}) collective-permute-start(bf16[3,8,128,128]{3,2,1,0:T(8,128)(2,1)S(1)} %slice.516), channel_id=1, source_target_pairs={{0,4},{4,0},{1,5},{5,1},{2,6},{6,2},{3,7},{7,3},{8,12},{12,8},{9,1... | collective-permute-start | bytes 2359304 | tf_op jit(solution)/shard_map/ppermute | solution.py:16
  39.1 0.2 fusion.57
  39.3 0.2 fusion.56
  39.5 0.4 collective-permute-start.5
  39.9 0.2 fusion.20
  40.1 19.1 %collective-permute-done.5 = f32[2,128,128]{2,1,0:T(8,128)S(1)} collective-permute-done((f32[2,128,128]{2,1,0:T(8,128)S(1)}, f32[2,128,128]{2,1,0:T(8,128)S(1)}, u32[]{:S(2)}, u32[]{:S(2)}) %collective-permute-start.5) | collective-permute-done | bytes 131104 | tf_op jit(solution)/shard_map/ppermute | solution.py:16
  59.2 0.1 slice_add_fusion.3
  59.4 0.2 fusion.48
  59.6 0.2 fusion.47
  59.8 1.6 %collective-permute-start.6 = (bf16[2,8,128,128]{3,2,1,0:T(8,128)(2,1)S(1)}, bf16[2,8,128,128]{3,2,1,0:T(8,128)(2,1)S(1)}, u32[]{:S(2)}, u32[]{:S(2)}) collective-permute-start(bf16[2,8,128,128]{3,2,1,0:T(8,128)(2,1)S(1)} %slice.526), channel_id=1, source_target_pairs={{0,8},{8,0},{1,9},{9,1},{2,10},{10,2},{3,11},{11,3},{4,12},{12,4},... | collective-permute-start | bytes 1572872 | tf_op jit(solution)/shard_map/ppermute | solution.py:16
  61.4 0.6 collective-permute-start.7
  62.0 0.2 fusion.18
  62.2 13.1 %collective-permute-done.7 = f32[2,128,128]{2,1,0:T(8,128)S(1)} collective-permute-done((f32[2,128,128]{2,1,0:T(8,128)S(1)}, f32[2,128,128]{2,1,0:T(8,128)S(1)}, u32[]{:S(2)}, u32[]{:S(2)}) %collective-permute-start.7) | collective-permute-done | bytes 131104 | tf_op jit(solution)/shard_map/ppermute | solution.py:16
  75.3 0.2 fusion.35
  75.5 0.2 fusion.39
  75.7 0.2 convolution_bitcast_fusion
  75.9 0.2 fusion.34
  76.1 2.3 %collective-permute-start.8 = (bf16[1,8,128,128]{3,2,1,0:T(8,128)(2,1)S(1)}, bf16[1,8,128,128]{3,2,1,0:T(8,128)(2,1)S(1)}, u32[]{:S(2)}, u32[]{:S(2)}) collective-permute-start(bf16[1,8,128,128]{3,2,1,0:T(8,128)(2,1)S(1)} %slice.536), channel_id=1, source_target_pairs={{0,16},{16,0},{1,17},{17,1},{2,18},{18,2},{3,19},{19,3},{4,20},{20... | collective-permute-start | bytes 786440 | tf_op jit(solution)/shard_map/ppermute | solution.py:16
  78.5 0.7 collective-permute-start.9
  79.2 0.2 fusion.16
  79.4 12.7 %collective-permute-done.8 = bf16[1,8,128,128]{3,2,1,0:T(8,128)(2,1)S(1)} collective-permute-done((bf16[1,8,128,128]{3,2,1,0:T(8,128)(2,1)S(1)}, bf16[1,8,128,128]{3,2,1,0:T(8,128)(2,1)S(1)}, u32[]{:S(2)}, u32[]{:S(2)}) %collective-permute-start.8) | collective-permute-done | bytes 262176 | tf_op jit(solution)/shard_map/ppermute | solution.py:16
  92.1 2.3 %collective-permute-done.9 = f32[2,128,128]{2,1,0:T(8,128)S(1)} collective-permute-done((f32[2,128,128]{2,1,0:T(8,128)S(1)}, f32[2,128,128]{2,1,0:T(8,128)S(1)}, u32[]{:S(2)}, u32[]{:S(2)}) %collective-permute-start.9) | collective-permute-done | bytes 131104 | tf_op jit(solution)/shard_map/ppermute | solution.py:16
  94.4 0.2 fusion.14
  94.6 0.2 convolution_add_fusion.1
  94.8 0.2 fusion.43
  95.0 0.2 fusion.33
  95.2 0.2 convolution_add_fusion.2
  95.4 0.2 fusion.52
  95.6 0.2 fusion.32
  95.8 0.2 convolution_add_fusion.3
  96.0 0.2 fusion.61
  96.1 0.2 fusion.31
  96.4 0.2 convolution_add_fusion.4
  96.5 0.2 fusion.78
  96.8 0.2 fusion.76
  97.1 0.2 convolution_add_fusion.5
  97.2 0.3 fusion.13
  97.5 0.3 fusion.1
  97.8 1.6 %fusion = f32[2,512,512]{2,1,0:T(8,128)S(1)} fusion(bf16[2,128,128]{2,1,0:T(8,128)(2,1)S(1)} %fusion.1, bf16[2,2,512,128]{3,2,1,0:T(8,128)(2,1)} %param.10), kind=kOutput, calls=%fused_computation.3 | convolution fusion | flops 167903232 | bytes 2686976 | tf_op jit(solution)/shard_map/lms,lns->lmn/dot_general | solution.py:104
  99.4 2.9 %add_convert_fusion = bf16[2,512,512]{2,1,0:T(8,128)(2,1)} fusion(f32[2,512,512]{2,1,0:T(8,128)S(1)} %fusion, bf16[2,512,512]{2,1,0:T(8,128)(2,1)S(1)} %copy-done, bf16[2,512,512]{2,1,0:T(8,128)(2,1)} %param.8), kind=kOutput, calls=%fused_computation | convolution fusion | flops 537919488 | bytes 5242880 | tf_op jit(solution)/shard_map/lij,ljk->lik/dot_general | solution.py:103
  (32 shorter events, 0.6 us)
Async XLA Ops:
  0.0 99.4 %copy-start = (bf16[2,512,512]{2,1,0:T(8,128)(2,1)S(1)}, bf16[2,512,512]{2,1,0:T(8,128)(2,1)}, u32[]{:S(2)}) copy-start(bf16[2,512,512]{2,1,0:T(8,128)(2,1)} %param.7) | copy-start | bytes 3145732
  1.9 2.8 %copy-start.2 = (bf16[1,4,2,128,128]{4,3,2,1,0:T(8,128)(2,1)S(1)}, bf16[1,4,2,128,128]{4,3,2,1,0:T(8,128)(2,1)}, u32[]{:S(2)}) copy-start(bf16[1,4,2,128,128]{4,3,2,1,0:T(8,128)(2,1)} %param.11) | copy-start | bytes 786436
  2.9 1.8 %copy-start.1 = (bf16[2,2,512,128]{3,2,1,0:T(8,128)(2,1)S(1)}, bf16[2,2,512,128]{3,2,1,0:T(8,128)(2,1)}, u32[]{:S(2)}) copy-start(bf16[2,2,512,128]{3,2,1,0:T(8,128)(2,1)} %param.9) | copy-start | bytes 1572868
  4.2 3.4 %collective-permute-start = (bf16[5,8,128,128]{3,2,1,0:T(8,128)(2,1)}, bf16[5,8,128,128]{3,2,1,0:T(8,128)(2,1)S(1)}, u32[]{:S(2)}, u32[]{:S(2)}) collective-permute-start(bf16[5,8,128,128]{3,2,1,0:T(8,128)(2,1)} %broadcast_select_fusion), channel_id=1, source_target_pairs={{0,1},{1,0},{2,3},{3,2},{4,5},{5,4},{6,7},{7,6},{8,9},{9,8},{10,11... | collective-permute-start | bytes 3932168 | tf_op jit(solution)/shard_map/ppermute | solution.py:16
  4.7 2.5 %copy-start.3 = (bf16[1,4,2,128,128]{4,3,2,1,0:T(8,128)(2,1)S(1)}, bf16[1,4,2,128,128]{4,3,2,1,0:T(8,128)(2,1)}, u32[]{:S(2)}) copy-start(bf16[1,4,2,128,128]{4,3,2,1,0:T(8,128)(2,1)} %param.12) | copy-start | bytes 786436
  6.1 4.8 %collective-permute-start.1 = (f32[2,128,128]{2,1,0:T(8,128)S(1)}, f32[2,128,128]{2,1,0:T(8,128)S(1)}, u32[]{:S(2)}, u32[]{:S(2)}) collective-permute-start(f32[2,128,128]{2,1,0:T(8,128)S(1)} %pad_maximum_fusion.1), channel_id=1, source_target_pairs={{0,1},{1,0},{2,3},{3,2},{4,5},{5,4},{6,7},{7,6},{8,9},{9,8},{10,11... | collective-permute-start | bytes 393224 | tf_op jit(solution)/shard_map/ppermute | solution.py:16
  7.9 29.2 %collective-permute-start.2 = (bf16[4,8,128,128]{3,2,1,0:T(8,128)(2,1)S(1)}, bf16[4,8,128,128]{3,2,1,0:T(8,128)(2,1)S(1)}, u32[]{:S(2)}, u32[]{:S(2)}) collective-permute-start(bf16[4,8,128,128]{3,2,1,0:T(8,128)(2,1)S(1)} %slice.506), channel_id=1, source_target_pairs={{0,2},{2,0},{1,3},{3,1},{4,6},{6,4},{5,7},{7,5},{8,10},{10,8},{9,1... | collective-permute-start | bytes 3145736 | tf_op jit(solution)/shard_map/ppermute | solution.py:16
  11.3 25.8 %collective-permute-start.3 = (f32[2,128,128]{2,1,0:T(8,128)S(1)}, f32[2,128,128]{2,1,0:T(8,128)S(1)}, u32[]{:S(2)}, u32[]{:S(2)}) collective-permute-start(f32[2,128,128]{2,1,0:T(8,128)S(1)} %pad_maximum_fusion.2), channel_id=1, source_target_pairs={{0,2},{2,0},{1,3},{3,1},{4,6},{6,4},{5,7},{7,5},{8,10},{10,8},{9,1... | collective-permute-start | bytes 393224 | tf_op jit(solution)/shard_map/ppermute | solution.py:16
  37.3 21.9 %collective-permute-start.4 = (bf16[3,8,128,128]{3,2,1,0:T(8,128)(2,1)S(1)}, bf16[3,8,128,128]{3,2,1,0:T(8,128)(2,1)S(1)}, u32[]{:S(2)}, u32[]{:S(2)}) collective-permute-start(bf16[3,8,128,128]{3,2,1,0:T(8,128)(2,1)S(1)} %slice.516), channel_id=1, source_target_pairs={{0,4},{4,0},{1,5},{5,1},{2,6},{6,2},{3,7},{7,3},{8,12},{12,8},{9,1... | collective-permute-start | bytes 2359304 | tf_op jit(solution)/shard_map/ppermute | solution.py:16
  39.5 19.7 %collective-permute-start.5 = (f32[2,128,128]{2,1,0:T(8,128)S(1)}, f32[2,128,128]{2,1,0:T(8,128)S(1)}, u32[]{:S(2)}, u32[]{:S(2)}) collective-permute-start(f32[2,128,128]{2,1,0:T(8,128)S(1)} %pad_maximum_fusion.3), channel_id=1, source_target_pairs={{0,4},{4,0},{1,5},{5,1},{2,6},{6,2},{3,7},{7,3},{8,12},{12,8},{9,1... | collective-permute-start | bytes 393224 | tf_op jit(solution)/shard_map/ppermute | solution.py:16
  59.8 15.4 %collective-permute-start.6 = (bf16[2,8,128,128]{3,2,1,0:T(8,128)(2,1)S(1)}, bf16[2,8,128,128]{3,2,1,0:T(8,128)(2,1)S(1)}, u32[]{:S(2)}, u32[]{:S(2)}) collective-permute-start(bf16[2,8,128,128]{3,2,1,0:T(8,128)(2,1)S(1)} %slice.526), channel_id=1, source_target_pairs={{0,8},{8,0},{1,9},{9,1},{2,10},{10,2},{3,11},{11,3},{4,12},{12,4},... | collective-permute-start | bytes 1572872 | tf_op jit(solution)/shard_map/ppermute | solution.py:16
  61.4 13.8 %collective-permute-start.7 = (f32[2,128,128]{2,1,0:T(8,128)S(1)}, f32[2,128,128]{2,1,0:T(8,128)S(1)}, u32[]{:S(2)}, u32[]{:S(2)}) collective-permute-start(f32[2,128,128]{2,1,0:T(8,128)S(1)} %pad_maximum_fusion.4), channel_id=1, source_target_pairs={{0,8},{8,0},{1,9},{9,1},{2,10},{10,2},{3,11},{11,3},{4,12},{12,4},... | collective-permute-start | bytes 393224 | tf_op jit(solution)/shard_map/ppermute | solution.py:16
  76.1 15.9 %collective-permute-start.8 = (bf16[1,8,128,128]{3,2,1,0:T(8,128)(2,1)S(1)}, bf16[1,8,128,128]{3,2,1,0:T(8,128)(2,1)S(1)}, u32[]{:S(2)}, u32[]{:S(2)}) collective-permute-start(bf16[1,8,128,128]{3,2,1,0:T(8,128)(2,1)S(1)} %slice.536), channel_id=1, source_target_pairs={{0,16},{16,0},{1,17},{17,1},{2,18},{18,2},{3,19},{19,3},{4,20},{20... | collective-permute-start | bytes 786440 | tf_op jit(solution)/shard_map/ppermute | solution.py:16
  78.5 15.9 %collective-permute-start.9 = (f32[2,128,128]{2,1,0:T(8,128)S(1)}, f32[2,128,128]{2,1,0:T(8,128)S(1)}, u32[]{:S(2)}, u32[]{:S(2)}) collective-permute-start(f32[2,128,128]{2,1,0:T(8,128)S(1)} %pad_maximum_fusion.5), channel_id=1, source_target_pairs={{0,16},{16,0},{1,17},{17,1},{2,18},{18,2},{3,19},{19,3},{4,20},{20... | collective-permute-start | bytes 393224 | tf_op jit(solution)/shard_map/ppermute | solution.py:16
where the time goes:
time: 103 us; the launch traced here: 102 us
  waiting for transfers between devices  73 us (71%)
  matrix products  12.7 us (12%)
  starting transfers between devices  11 us (11%)
  local copies, waits for them, and re-layouts  3.06 us (3%)
  other arithmetic  2.01 us (2%)
    ppermute x10, waiting for transfers between devices, from_partner(): return lax.ppermute(block, axis, route)  73 us
    ppermute x10, starting transfers between devices, from_partner(): return lax.ppermute(block, axis, route)  11 us
    dot_general x38, matrix products, multiply(): jnp.matmul(first_arg.astype(jnp.float32), second_arg.astype(jnp.float32),...  7.96 us
    dot_general x1, matrix products, shards(): jnp.einsum('lij,ljk->lik', dense_a, dense_b, preferred_element_type=jnp.f...  2.91 us
  transfers between devices with their start and end apart: 10, of which 6 were waited for; matrix products, arithmetic and copies ran while one was open for 4% of the time, Pallas kernels for 0%

commit v1 on v0

v1 whole, which is shorter than its diff:
```python
import functools

import jax
import jax.numpy as jnp
from jax import lax
from jax.experimental import pallas as pl
from jax.experimental.pallas import tpu as pltpu
from jax.sharding import PartitionSpec as P

MESH = pl.DeviceIdType.MESH
BF16 = jnp.bfloat16
F32 = jnp.float32
ASC, DESC, COUP = 0, 1, 2


def mm(a, b, ca=1, cb=0):
    return lax.dot_general(
        a.astype(BF16), b.astype(BF16), (((ca,), (cb,)), ((), ())), preferred_element_type=F32
    )


def halves(value):
    high = value.astype(BF16)
    return high, (value - high.astype(F32)).astype(BF16)


def times(value, factor, cb=0):
    if value.dtype == BF16:
        return mm(value, factor, 1, cb)
    rows = value.shape[0]
    both = mm(jnp.concatenate(halves(value), 0), factor, 1, cb)
    return both[:rows] + both[rows:]


def into(factor, value, ca=1):
    if value.dtype == BF16:
        return mm(factor, value, ca, 0)
    columns = value.shape[1]
    both = mm(factor, jnp.concatenate(halves(value), 1), ca, 0)
    return both[:, :columns] + both[:, columns:]


def lift(pair, value):
    return into(pair[0], times(value, pair[1]), 0)


def lower(pair, value):
    return times(into(pair[0], value), pair[1], 1)


def across(first, value, second):
    return times(into(first, value), second)


def tree_kernel(
    levels, columns,
    da_ref, db_ref, inner_ref, outer_ref, asc_ref, desc_ref, coup_ref, o_ref,
    da, db, inner, outer, own_asc, own_desc, own_coup, out, dense,
    table, f_out, t_out, f_in, t_in, near_leaf, near_up,
    load_sem, out_sem, gen_send, gen_recv, up_send, up_recv,
):
    pos = lax.axis_index("row") * columns + lax.axis_index("col")
    bit = [pos // 2**i % 2 for i in range(levels)]
    partner = []
    for i in range(levels):
        other = pos + 2**i * (1 - 2 * bit[i])
        partner.append((other // columns, other % columns))

    low_sum = {}
    for h in range(1, levels + 1):
        total = 0
        for i in range(h):
            total = total + (bit[i] if i == h - 1 else 1 - bit[i])
            low_sum[h, i] = total
    count = {h: low_sum[h, h - 1] for h in range(1, levels + 1)}
    last = {ASC: levels - 2, DESC: levels - 2, COUP: levels}

    barrier = pltpu.get_barrier_semaphore()
    for i in range(levels):
        pl.semaphore_signal(barrier, inc=1, device_id=partner[i], device_id_type=MESH)

    loads = [
        pltpu.make_async_copy(src, dst, load_sem.at[n])
        for n, (src, dst) in enumerate([
            (inner_ref, inner),
            (asc_ref.at[0], own_asc),
            (coup_ref.at[0, 0], own_coup),
            (desc_ref.at[0], own_desc),
            (outer_ref, outer),
            (da_ref, da),
            (db_ref, db),
        ])
    ]
    for copy in loads[:4]:
        copy.start()

    def slot(kind, h):
        return table.at[kind, h]

    def own_source(kind):
        return (asc_ref if kind == ASC else desc_ref).at[0, 3]

    def send(kind, h, i, src):
        return pltpu.make_async_remote_copy(
            src_ref=src, dst_ref=slot(kind, h),
            send_sem=gen_send.at[kind, h, i], recv_sem=gen_recv.at[kind, h],
            device_id=partner[i], device_id_type=MESH,
        )

    def wait_slot(kind, h):
        pltpu.make_async_copy(slot(kind, h), slot(kind, h), gen_recv.at[kind, h]).wait()

    def owner_local(kind, h):
        if kind == COUP:
            for n, k in enumerate((0, 3)):
                pltpu.make_async_copy(
                    coup_ref.at[0, 1, k], table.at[COUP, h, n], gen_recv.at[COUP, h]
                ).start()
        else:
            pltpu.make_async_copy(own_source(kind), slot(kind, h), gen_recv.at[kind, h]).start()

    pl.semaphore_wait(barrier, levels)

    for h in range(1, levels + 1):
        @pl.when(count[h] == 0)
        def _(h=h):
            for kind in (ASC, DESC, COUP):
                if h > last[kind]:
                    continue
                if kind == COUP:
                    send(kind, h, h - 1, coup_ref.at[0, 1, 1:3]).start()
                else:
                    for i in reversed(range(h)):
                        send(kind, h, i, own_source(kind)).start()
                owner_local(kind, h)

    def forwards(k, kinds):
        for kind in kinds:
            for h in range(2, last[kind] + 1):
                if k > h - 1 or (k == 0 and kind != COUP):
                    continue

                @pl.when((count[h] == k) & (low_sum[h, 0] == 0))
                def _(kind=kind, h=h):
                    wait_slot(kind, h)
                    for i in reversed(range(h - 1)):
                        @pl.when(low_sum[h, i] == 0)
                        def _(i=i):
                            send(kind, h, i, slot(kind, h)).start()

    def ready(kind, h):
        if h == 1:
            wait_slot(kind, h)
            return
        waited = low_sum[h, 0] == 0
        if kind != COUP:
            waited = waited & (count[h] > 0)

        @pl.when(jnp.logical_not(waited))
        def _():
            wait_slot(kind, h)

    def up_copy(which, h):
        src, dst = ((f_out, f_in), (t_out, t_in))[which]
        return pltpu.make_async_remote_copy(
            src_ref=src.at[h], dst_ref=dst.at[h],
            send_sem=up_send.at[which, h], recv_sem=up_recv.at[which, h],
            device_id=partner[h], device_id_type=MESH,
        )

    def near(h):
        ready(COUP, h)
        up_copy(0, h - 1).wait()
        pair = slot(COUP, h)
        return across(pair[0], f_in[h - 1], pair[1])

    for copy in loads[4:]:
        copy.start()
    loads[0].wait()
    leaf = [mm(inner[u, 0], inner[u, 1], 0, 0) for u in range(2)]
    loads[1].wait()
    node = lift(own_asc.at[0], leaf[0]) + lift(own_asc.at[1], leaf[1])
    done = 0
    for h in range(levels):
        f_out[h] = node.astype(BF16)
        up_copy(0, h).start()
        if h < levels - 1:
            if h == 0:
                pair = own_asc.at[2]
            else:
                ready(ASC, h)
                pair = slot(ASC, h)
            term = lift(pair, node)
            t_out[h] = term.astype(BF16)
            up_copy(1, h).start()
        if h == 0:
            loads[2].wait()
            near_leaf[0] = across(own_coup[0], leaf[1], own_coup[3])
            near_leaf[1] = across(own_coup[1], leaf[0], own_coup[2])
        if h == min(1, levels - 1):
            loads[5].wait()
            loads[6].wait()
            for u in range(2):
                dense[u] = mm(da[u], db[u])
        forwards(h + 1, (ASC,))
        forwards(h, (DESC, COUP))
        while done < h - 1:
            done += 1
            near_up[done - 1] = near(done)
        if h < levels - 1:
            up_copy(1, h).wait()
            node = term + t_in[h].astype(F32)

    loads[3].wait()
    loads[4].wait()
    while done < levels - 1:
        done += 1
        near_up[done - 1] = near(done)
    for h in range(1, levels - 1):
        ready(DESC, h)
    coupling = near(levels)
    for h in range(levels - 2, -1, -1):
        pair = slot(DESC, h) if h else own_desc.at[2]
        coupling = near_up[h] + lower(pair, coupling)
    stores = []
    for u in range(2):
        value = (near_leaf[u] + lower(own_desc.at[u], coupling)).astype(BF16)
        spread = mm(outer[u, 0], value).astype(BF16)
        out[u] = (dense[u] + mm(spread, outer[u, 1], 1, 1)).astype(BF16)
        store = pltpu.make_async_copy(out.at[u], o_ref.at[u], out_sem.at[u])
        store.start()
        stores.append(store)

    for h in range(1, levels + 1):
        for kind in (ASC, DESC, COUP):
            if h > last[kind]:
                continue
            for i in range(h):
                if i == h - 1:
                    sent = count[h] == 0
                else:
                    sent = low_sum[h, i] == 0

                @pl.when(sent)
                def _(kind=kind, h=h, i=i):
                    send(kind, h, i, slot(kind, h)).wait_send()
    for store in stores:
        store.wait()


def shards(levels, columns, dense_a, dense_b, inner, outer, ascent, descent, couplings):
    r = ascent.shape[-1]
    anywhere = pl.BlockSpec(memory_space=pl.ANY)
    vmem = pltpu.VMEM
    dma = pltpu.SemaphoreType.DMA
    return pl.pallas_call(
        functools.partial(tree_kernel, levels, columns),
        out_shape=jax.ShapeDtypeStruct(dense_a.shape, BF16),
        in_specs=[anywhere] * 7,
        out_specs=anywhere,
        scratch_shapes=[
            vmem(dense_a.shape, BF16),
            vmem(dense_b.shape, BF16),
            vmem(inner.shape, BF16),
            vmem(outer.shape, BF16),
            vmem(ascent.shape[1:], BF16),
            vmem(descent.shape[1:], BF16),
            vmem(couplings.shape[2:], BF16),
            vmem(dense_a.shape, BF16),
            vmem(dense_a.shape, F32),
            vmem((3, levels + 1, 2, r, r), BF16),
            vmem((levels, r, r), BF16),
            vmem((levels, r, r), BF16),
            vmem((levels, r, r), BF16),
            vmem((levels, r, r), BF16),
            vmem((2, r, r), F32),
            vmem((levels, r, r), F32),
            dma((7,)),
            dma((2,)),
            dma((3, levels + 1, levels)),
            dma((3, levels + 1)),
            dma((2, levels)),
            dma((2, levels)),
        ],
        compiler_params=pltpu.CompilerParams(collective_id=0, has_side_effects=True),
    )(dense_a, dense_b, inner, outer, ascent, descent, couplings)


def solution(mesh):
    rows, columns = mesh.shape["row"], mesh.shape["col"]
    levels = (rows * columns).bit_length() - 1
    both = ("row", "col")
    placed = (
        P(both, None, None),
        P(both, None, None),
        P(both, None, None, None),
        P(both, None, None, None),
        P(both, None, None, None, None),
        P(both, None, None, None, None),
        P(both, None, None, None, None),
    )
    return jax.shard_map(
        functools.partial(shards, levels, columns),
        mesh=mesh, in_specs=placed, out_specs=P(both, None, None), check_vma=False,
    )
```

time: 103 us -> 28.1 us (0.27)
  waiting for transfers between devices: 73 us -> 0 us
  Pallas kernels: 0 us -> 25.7 us
  matrix products: 12.7 us -> 0 us
  starting transfers between devices: 11 us -> 0 us
  other arithmetic: 2.01 us -> 0 us
    ppermute x10 -> x0, waiting for transfers between devices: 73 us -> none  [from_partner(): return lax.ppermute(block, axis, route)]
    pallas_call x0 -> x1, Pallas kernels: none -> 25.7 us  [shards(): pl.pallas_call(functools.partial(tree_kernel, levels, columns), out_shape...]
    dot_general x41 -> x0, matrix products: 12.7 us -> none  [the longest x38 7.96 us: multiply(): jnp.matmul(first_arg.astype(jnp.float32), second_arg.astype(jnp.float32),...]
    ppermute x10 -> x0, starting transfers between devices: 11 us -> none  [from_partner(): return lax.ppermute(block, axis, route)]
    unnamed x8 -> x1, local copies, waits for them, and re-layouts: 0.02 us -> 2.26 us
    squeeze x2 -> x0, local copies, waits for them, and re-layouts: 1.76 us -> none  [shards(): own_gens = jnp.concatenate([up_pairs[3], down_pairs[3], blocks[1]], 0)]
    slice x7 -> x0, local copies, waits for them, and re-layouts: 1.28 us -> none  [the longest x1 1.03 us: shards(): near_leaves = sibling_terms(blocks[0][None], leaf_inner_product)]
    select_n x1 -> x0, other arithmetic: 1.24 us -> none  [shards(): table = jnp.where(holder, own_gens[None], jnp.zeros_like(own_gens)[None])]
  transfers between devices with their start and end apart: 10 -> 0, of which waited for: 6 -> 0; matrix products, arithmetic and copies ran while one was open for 4% -> 0% of each run, Pallas kernels for 0% -> 0%
where the time goes in v1:
time: 28.1 us; the launch traced here: 28 us
  Pallas kernels  25.7 us (91%)
  local copies, waits for them, and re-layouts  2.26 us (8%)
    pallas_call x1, Pallas kernels, shards(): pl.pallas_call(functools.partial(tree_kernel, levels, columns), out_shape...  25.7 us
    unnamed x1, local copies, waits for them, and re-layouts  2.26 us

profile of v1, /device:TPU:0, one launch (start us, length us, event | category | flops | bytes accessed | tf_op | source)
XLA Modules:
  0.0 28.0 jit_solution(4706350268474053167)
XLA Ops:
  0.0 25.7 %shard_map.73 = bf16[2,512,512]{2,1,0:T(8,128)(2,1)} custom-call(bf16[2,512,512]{2,1,0:T(8,128)(2,1)} %da_ref.1, bf16[2,512,512]{2,1,0:T(8,128)(2,1)} %db_ref.1, bf16[2,2,512,128]{3,2,1,0:T(8,128)(2,1)} %inner_ref.1, bf16[2,2,512,128]{3,2,1,0:T(8,128)(2,1)} %outer_ref.1, bf16[1,4,2,128,128]{4,3,2,1,0:T(8,128)(2,1)} %asc_ref.1, ...), custom_call_target="tpu_custom_call" | custom-call | tf_op jit(solution)/shard_map/pallas_call | solution.py:256
  25.7 2.3 %copy.9 = bf16[2,512,512]{2,1,0:T(8,128)(2,1)} copy(bf16[2,512,512]{2,1,0:T(8,128)(2,1)} %shard_map.73) | data formatting | bytes 2097152

commit v2 on v1

--- a/solution.py
+++ b/solution.py
@@ -57,7 +57,8 @@
     da_ref, db_ref, inner_ref, outer_ref, asc_ref, desc_ref, coup_ref, o_ref,
     da, db, inner, outer, own_asc, own_desc, own_coup, out, dense,
     table, f_out, t_out, f_in, t_in, near_leaf, near_up,
-    load_sem, out_sem, gen_send, gen_recv, up_send, up_recv,
+    comp, far_in,
+    load_sem, out_sem, gen_send, gen_recv, up_send, up_recv, far_send, far_recv,
 ):
     pos = lax.axis_index("row") * columns + lax.axis_index("col")
     bit = [pos // 2**i % 2 for i in range(levels)]
@@ -65,6 +66,11 @@
     for i in range(levels):
         other = pos + 2**i * (1 - 2 * bit[i])
         partner.append((other // columns, other % columns))
+
+    top = levels - 1
+    far = pos + 2**top * (1 - 2 * bit[top])
+    cross = far + 2 ** (top - 1) * (1 - 2 * bit[top - 1])
+    opposite = (partner[top], (cross // columns, cross % columns))
 
     low_sum = {}
     for h in range(1, levels + 1):
@@ -76,8 +82,8 @@
     last = {ASC: levels - 2, DESC: levels - 2, COUP: levels}
 
     barrier = pltpu.get_barrier_semaphore()
-    for i in range(levels):
-        pl.semaphore_signal(barrier, inc=1, device_id=partner[i], device_id_type=MESH)
+    for other in [*partner, opposite[1]]:
+        pl.semaphore_signal(barrier, inc=1, device_id=other, device_id_type=MESH)
 
     loads = [
         pltpu.make_async_copy(src, dst, load_sem.at[n])
@@ -119,7 +125,62 @@
         else:
             pltpu.make_async_copy(own_source(kind), slot(kind, h), gen_recv.at[kind, h]).start()
 
-    pl.semaphore_wait(barrier, levels)
+    def forwards(k, kinds):
+        for kind in kinds:
+            for h in range(2, last[kind] + 1):
+                if k > h - 1 or (k == 0 and kind != COUP):
+                    continue
+
+                @pl.when((count[h] == k) & (low_sum[h, 0] == 0))
+                def _(kind=kind, h=h):
+                    wait_slot(kind, h)
+                    for i in reversed(range(h - 1)):
+                        @pl.when(low_sum[h, i] == 0)
+                        def _(i=i):
+                            send(kind, h, i, slot(kind, h)).start()
+
+    def ready(kind, h):
+        if h == 1:
+            wait_slot(kind, h)
+            return
+        waited = low_sum[h, 0] == 0
+        if kind != COUP:
+            waited = waited & (count[h] > 0)
+
+        @pl.when(jnp.logical_not(waited))
+        def _():
+            wait_slot(kind, h)
+
+    def up_copy(which, h):
+        src, dst = ((f_out, f_in), (t_out, t_in))[which]
+        return pltpu.make_async_remote_copy(
+            src_ref=src.at[h], dst_ref=dst.at[h],
+            send_sem=up_send.at[which, h], recv_sem=up_recv.at[which, h],
+            device_id=partner[h], device_id_type=MESH,
+        )
+
+    def near(h):
+        ready(COUP, h)
+        up_copy(0, h - 1).wait()
+        pair = slot(COUP, h)
+        return across(pair[0], f_in[h - 1], pair[1])
+
+    def far_copy(n):
+        return pltpu.make_async_remote_copy(
+            src_ref=t_out.at[top - 1], dst_ref=far_in.at[n],
+            send_sem=far_send.at[n], recv_sem=far_recv.at[n],
+            device_id=opposite[n], device_id_type=MESH,
+        )
+
+    def compose(n, left, right, h):
+        ready(COUP, h)
+        pair = slot(COUP, h)
+        for u in range(2):
+            comp[n, 0, u] = times(into(own_desc[u, 0], left), pair[0]).astype(BF16)
+            high, low = halves(into(own_desc[u, 1], right))
+            comp[n, 1, u] = (mm(pair[1], high, 1, 1) + mm(pair[1], low, 1, 1)).astype(BF16)
+
+    pl.semaphore_wait(barrier, levels + 1)
 
     for h in range(1, levels + 1):
         @pl.when(count[h] == 0)
@@ -134,70 +195,35 @@
                         send(kind, h, i, own_source(kind)).start()
                 owner_local(kind, h)
 
-    def forwards(k, kinds):
-        for kind in kinds:
-            for h in range(2, last[kind] + 1):
-                if k > h - 1 or (k == 0 and kind != COUP):
-                    continue
-
-                @pl.when((count[h] == k) & (low_sum[h, 0] == 0))
-                def _(kind=kind, h=h):
-                    wait_slot(kind, h)
-                    for i in reversed(range(h - 1)):
-                        @pl.when(low_sum[h, i] == 0)
-                        def _(i=i):
-                            send(kind, h, i, slot(kind, h)).start()
-
-    def ready(kind, h):
-        if h == 1:
-            wait_slot(kind, h)
-            return
-        waited = low_sum[h, 0] == 0
-        if kind != COUP:
-            waited = waited & (count[h] > 0)
-
-        @pl.when(jnp.logical_not(waited))
-        def _():
-            wait_slot(kind, h)
-
-    def up_copy(which, h):
-        src, dst = ((f_out, f_in), (t_out, t_in))[which]
-        return pltpu.make_async_remote_copy(
-            src_ref=src.at[h], dst_ref=dst.at[h],
-            send_sem=up_send.at[which, h], recv_sem=up_recv.at[which, h],
-            device_id=partner[h], device_id_type=MESH,
-        )
-
-    def near(h):
-        ready(COUP, h)
-        up_copy(0, h - 1).wait()
-        pair = slot(COUP, h)
-        return across(pair[0], f_in[h - 1], pair[1])
-
+    loads[0].wait()
     for copy in loads[4:]:
         copy.start()
-    loads[0].wait()
     leaf = [mm(inner[u, 0], inner[u, 1], 0, 0) for u in range(2)]
     loads[1].wait()
     node = lift(own_asc.at[0], leaf[0]) + lift(own_asc.at[1], leaf[1])
+    term = lift(own_asc.at[2], node)
+    f_out[0] = node.astype(BF16)
+    t_out[0] = term.astype(BF16)
+
     done = 0
-    for h in range(levels):
-        f_out[h] = node.astype(BF16)
+    for h in range(top):
+        if h > 0:
+            ready(ASC, h)
+            term = lift(slot(ASC, h), node)
+            t_out[h] = term.astype(BF16)
+        if h < top - 1:
+            up_copy(1, h).start()
+        else:
+            far_copy(1).start()
+            far_copy(0).start()
+        if h > 0:
+            f_out[h] = node.astype(BF16)
         up_copy(0, h).start()
-        if h < levels - 1:
-            if h == 0:
-                pair = own_asc.at[2]
-            else:
-                ready(ASC, h)
-                pair = slot(ASC, h)
-            term = lift(pair, node)
-            t_out[h] = term.astype(BF16)
-            up_copy(1, h).start()
         if h == 0:
             loads[2].wait()
             near_leaf[0] = across(own_coup[0], leaf[1], own_coup[3])
             near_leaf[1] = across(own_coup[1], leaf[0], own_coup[2])
-        if h == min(1, levels - 1):
+        if h == min(1, top - 1):
             loads[5].wait()
             loads[6].wait()
             for u in range(2):
@@ -207,24 +233,41 @@
         while done < h - 1:
             done += 1
             near_up[done - 1] = near(done)
-        if h < levels - 1:
+        if h < top - 1:
             up_copy(1, h).wait()
             node = term + t_in[h].astype(F32)
 
+    for k in range(top, levels):
+        forwards(k, (DESC, COUP))
     loads[3].wait()
     loads[4].wait()
-    while done < levels - 1:
+    while done < top - 1:
         done += 1
         near_up[done - 1] = near(done)
-    for h in range(1, levels - 1):
+    for h in range(1, top):
         ready(DESC, h)
-    coupling = near(levels)
-    for h in range(levels - 2, -1, -1):
-        pair = slot(DESC, h) if h else own_desc.at[2]
-        coupling = near_up[h] + lower(pair, coupling)
+    coupling = near_up[top - 2]
+    for h in range(top - 3, -1, -1):
+        coupling = near_up[h] + lower(slot(DESC, h) if h else own_desc.at[2], coupling)
+    for u in range(2):
+        near_leaf[u] += lower(own_desc.at[u], coupling)
+
+    left, right = own_desc[2, 0], own_desc[2, 1]
+    for h in range(1, top - 1):
+        left, right = times(left, table[DESC, h, 0]), times(right, table[DESC, h, 1])
+    compose(0, left, right, top)
+    left, right = times(left, table[DESC, top - 1, 0]), times(right, table[DESC, top - 1, 1])
+    compose(1, left, right, levels)
+
+    up_copy(0, top - 1).wait()
+    for u in range(2):
+        near_leaf[u] += mm(mm(comp[0, 0, u], f_in[top - 1]), comp[0, 1, u])
+    for n in (0, 1):
+        far_copy(n).wait()
+    last_inner = (far_in[0].astype(F32) + far_in[1].astype(F32)).astype(BF16)
     stores = []
     for u in range(2):
-        value = (near_leaf[u] + lower(own_desc.at[u], coupling)).astype(BF16)
+        value = (near_leaf[u] + mm(mm(comp[1, 0, u], last_inner), comp[1, 1, u])).astype(BF16)
         spread = mm(outer[u, 0], value).astype(BF16)
         out[u] = (dense[u] + mm(spread, outer[u, 1], 1, 1)).astype(BF16)
         store = pltpu.make_async_copy(out.at[u], o_ref.at[u], out_sem.at[u])
@@ -250,13 +293,14 @@
 
 def shards(levels, columns, dense_a, dense_b, inner, outer, ascent, descent, couplings):
     r = ascent.shape[-1]
+    arrays = (dense_a, dense_b, inner, outer, ascent, descent, couplings)
     anywhere = pl.BlockSpec(memory_space=pl.ANY)
     vmem = pltpu.VMEM
     dma = pltpu.SemaphoreType.DMA
     return pl.pallas_call(
         functools.partial(tree_kernel, levels, columns),
         out_shape=jax.ShapeDtypeStruct(dense_a.shape, BF16),
-        in_specs=[anywhere] * 7,
+        in_specs=[pl.BlockSpec(memory_space=pltpu.HBM)] * 7,
         out_specs=anywhere,
         scratch_shapes=[
             vmem(dense_a.shape, BF16),
@@ -275,15 +319,19 @@
             vmem((levels, r, r), BF16),
             vmem((2, r, r), F32),
             vmem((levels, r, r), F32),
+            vmem((2, 2, 2, r, r), BF16),
+            vmem((2, r, r), BF16),
             dma((7,)),
             dma((2,)),
             dma((3, levels + 1, levels)),
             dma((3, levels + 1)),
             dma((2, levels)),
             dma((2, levels)),
+            dma((2,)),
+            dma((2,)),
         ],
-        compiler_params=pltpu.CompilerParams(collective_id=0, has_side_effects=True),
-    )(dense_a, dense_b, inner, outer, ascent, descent, couplings)
+        compiler_params=pltpu.CompilerParams(collective_id=0, has_side_effects=True, vmem_limit_bytes=24 * 2**20),
+    )(*(pltpu.with_memory_space_constraint(x, pltpu.HBM) for x in arrays))
 
 
 def solution(mesh):

time: 28.1 us -> 22.8 us (0.81)
  Pallas kernels: 25.7 us -> 21.7 us
  local copies, waits for them, and re-layouts: 2.26 us -> 0.97 us
    pallas_call x1, Pallas kernels: 25.7 us -> 21.7 us  [shards(): pl.pallas_call(functools.partial(tree_kernel, levels, columns), out_shape...]
    unnamed x1, local copies, waits for them, and re-layouts: 2.26 us -> 0.97 us
where the time goes in v2:
time: 22.8 us; the launch traced here: 22.6 us
  Pallas kernels  21.7 us (95%)
  local copies, waits for them, and re-layouts  0.97 us (4%)
    pallas_call x1, Pallas kernels, shards(): pl.pallas_call(functools.partial(tree_kernel, levels, columns), out_shape...  21.7 us
    unnamed x1, local copies, waits for them, and re-layouts  0.97 us

profile of v2, /device:TPU:0, one launch (start us, length us, event | category | flops | bytes accessed | tf_op | source)
XLA Modules:
  0.0 22.6 jit_solution(17853827745502075454)
XLA Ops:
  0.0 21.7 %shard_map.73 = bf16[2,512,512]{2,1,0:T(8,128)(2,1)S(1)} custom-call(bf16[2,512,512]{2,1,0:T(8,128)(2,1)} %da_ref.1, bf16[2,512,512]{2,1,0:T(8,128)(2,1)} %db_ref.1, bf16[2,2,512,128]{3,2,1,0:T(8,128)(2,1)} %inner_ref.1, bf16[2,2,512,128]{3,2,1,0:T(8,128)(2,1)} %outer_ref.1, bf16[1,4,2,128,128]{4,3,2,1,0:T(8,128)(2,1)} %asc_ref.1, ...), custom_call_target="tpu_custom_call" | custom-call | tf_op jit(solution)/shard_map/pallas_call | solution.py:300
  21.7 1.0 %copy.9 = bf16[2,512,512]{2,1,0:T(8,128)(2,1)} copy(bf16[2,512,512]{2,1,0:T(8,128)(2,1)S(1)} %shard_map.73) | data formatting | bytes 2097152

commit v3 on v2

--- a/solution.py
+++ b/solution.py
@@ -55,10 +55,10 @@
 def tree_kernel(
     levels, columns,
     da_ref, db_ref, inner_ref, outer_ref, asc_ref, desc_ref, coup_ref, o_ref,
-    da, db, inner, outer, own_asc, own_desc, own_coup, out, dense,
+    da, db, inner, outer, own_asc, own_desc, own_coup, dense,
     table, f_out, t_out, f_in, t_in, near_leaf, near_up,
     comp, far_in,
-    load_sem, out_sem, gen_send, gen_recv, up_send, up_recv, far_send, far_recv,
+    load_sem, gen_send, gen_recv, up_send, up_recv, far_send, far_recv,
 ):
     pos = lax.axis_index("row") * columns + lax.axis_index("col")
     bit = [pos // 2**i % 2 for i in range(levels)]
@@ -223,13 +223,13 @@
             loads[2].wait()
             near_leaf[0] = across(own_coup[0], leaf[1], own_coup[3])
             near_leaf[1] = across(own_coup[1], leaf[0], own_coup[2])
-        if h == min(1, top - 1):
+        if h == 1:
             loads[5].wait()
             loads[6].wait()
-            for u in range(2):
-                dense[u] = mm(da[u], db[u])
+        if h in (1, 2):
+            dense[h - 1] = mm(da[h - 1], db[h - 1])
         forwards(h + 1, (ASC,))
-        forwards(h, (DESC, COUP))
+        forwards(h - 1, (DESC, COUP))
         while done < h - 1:
             done += 1
             near_up[done - 1] = near(done)
@@ -237,7 +237,7 @@
             up_copy(1, h).wait()
             node = term + t_in[h].astype(F32)
 
-    for k in range(top, levels):
+    for k in range(top - 1, levels):
         forwards(k, (DESC, COUP))
     loads[3].wait()
     loads[4].wait()
@@ -265,14 +265,10 @@
     for n in (0, 1):
         far_copy(n).wait()
     last_inner = (far_in[0].astype(F32) + far_in[1].astype(F32)).astype(BF16)
-    stores = []
     for u in range(2):
         value = (near_leaf[u] + mm(mm(comp[1, 0, u], last_inner), comp[1, 1, u])).astype(BF16)
         spread = mm(outer[u, 0], value).astype(BF16)
-        out[u] = (dense[u] + mm(spread, outer[u, 1], 1, 1)).astype(BF16)
-        store = pltpu.make_async_copy(out.at[u], o_ref.at[u], out_sem.at[u])
-        store.start()
-        stores.append(store)
+        o_ref[u] = (dense[u] + mm(spread, outer[u, 1], 1, 1)).astype(BF16)
 
     for h in range(1, levels + 1):
         for kind in (ASC, DESC, COUP):
@@ -287,21 +283,18 @@
                 @pl.when(sent)
                 def _(kind=kind, h=h, i=i):
                     send(kind, h, i, slot(kind, h)).wait_send()
-    for store in stores:
-        store.wait()
 
 
 def shards(levels, columns, dense_a, dense_b, inner, outer, ascent, descent, couplings):
     r = ascent.shape[-1]
     arrays = (dense_a, dense_b, inner, outer, ascent, descent, couplings)
-    anywhere = pl.BlockSpec(memory_space=pl.ANY)
     vmem = pltpu.VMEM
     dma = pltpu.SemaphoreType.DMA
     return pl.pallas_call(
         functools.partial(tree_kernel, levels, columns),
         out_shape=jax.ShapeDtypeStruct(dense_a.shape, BF16),
         in_specs=[pl.BlockSpec(memory_space=pltpu.HBM)] * 7,
-        out_specs=anywhere,
+        out_specs=pl.BlockSpec(memory_space=pltpu.VMEM),
         scratch_shapes=[
             vmem(dense_a.shape, BF16),
             vmem(dense_b.shape, BF16),
@@ -310,7 +303,6 @@
             vmem(ascent.shape[1:], BF16),
             vmem(descent.shape[1:], BF16),
             vmem(couplings.shape[2:], BF16),
-            vmem(dense_a.shape, BF16),
             vmem(dense_a.shape, F32),
             vmem((3, levels + 1, 2, r, r), BF16),
             vmem((levels, r, r), BF16),
@@ -322,7 +314,6 @@
             vmem((2, 2, 2, r, r), BF16),
             vmem((2, r, r), BF16),
             dma((7,)),
-            dma((2,)),
             dma((3, levels + 1, levels)),
             dma((3, levels + 1)),
             dma((2, levels)),

time: 22.8 us -> 22.4 us (0.982)
  the two profiles are of different devices: /device:TPU:0 before, /device:TPU:17 now
where the time goes in v3:
time: 22.4 us; the launch traced here: 22.3 us
  Pallas kernels  21.3 us (95%)
  local copies, waits for them, and re-layouts  0.97 us (4%)
    pallas_call x1, Pallas kernels, shards(): pl.pallas_call(functools.partial(tree_kernel, levels, columns), out_shape...  21.3 us
    unnamed x1, local copies, waits for them, and re-layouts  0.97 us

profile of v3, /device:TPU:17, one launch (start us, length us, event | category | flops | bytes accessed | tf_op | source)
XLA Modules:
  0.0 22.3 jit_solution(6785995447657029366)
XLA Ops:
  0.0 21.3 %shard_map.73 = bf16[2,512,512]{2,1,0:T(8,128)(2,1)S(1)} custom-call(bf16[2,512,512]{2,1,0:T(8,128)(2,1)} %da_ref.1, bf16[2,512,512]{2,1,0:T(8,128)(2,1)} %db_ref.1, bf16[2,2,512,128]{3,2,1,0:T(8,128)(2,1)} %inner_ref.1, bf16[2,2,512,128]{3,2,1,0:T(8,128)(2,1)} %outer_ref.1, bf16[1,4,2,128,128]{4,3,2,1,0:T(8,128)(2,1)} %asc_ref.1, ...), custom_call_target="tpu_custom_call" | custom-call | tf_op jit(solution)/shard_map/pallas_call | solution.py:293
  21.3 1.0 %copy.9 = bf16[2,512,512]{2,1,0:T(8,128)(2,1)} copy(bf16[2,512,512]{2,1,0:T(8,128)(2,1)S(1)} %shard_map.73) | data formatting | bytes 2097152
